TPU v7x, 256 devices: a whole 4x4x8 slice. The times are simulated.
256 devices in a mesh: row: 8 (over x, y_lo), blk: 32 (over y_hi, z, core).
Axes of the slice: x: 4, y: 4 (y_hi: 2, y_lo: 2; y = y_hi * 2 + y_lo), z: 8, core: 2. Of those that a mesh axis runs over, the one named last changes fastest.
Arguments:
- elastic_kernel: bfloat16 [32, 1024, 8, 4096], P('blk', None, 'row'), may hold values from -0.046875 to 0.046875
- slip_deficit: float32 [32, 8, 128, 512], P('blk', 'row'), may hold values from -6 to 6
- state_variable: float32 [32, 8, 128, 512], P('blk', 'row'), may hold values from 0.2 to 5
- step_size: float32 [512], replicated, may hold values from 0.02 to 0.1
- load_stress: float32 [32, 8, 128], P('blk', 'row'), may hold values from -6 to 6
- normal_stress: float32 [32, 8, 128], P('blk', 'row'), may hold values from 0.5 to 2
- rate_table: float32 [16], replicated, may hold values from 0.3 to 1
- evolve_table: float32 [16], replicated, may hold values from 0.3 to 1.5
- patch_region: int32 [32, 8, 128], P('blk', 'row'), may hold values from 0 to 15
- creep_flag: int32 [32, 8, 128], P('blk', 'row'), may hold values 0 or 1
Outputs:
- velocity: float32 [32, 8, 128, 512], P('blk', 'row')
- deficit_out: float32 [32, 8, 128, 512], P('blk', 'row')
- state_out: float32 [32, 8, 128, 512], P('blk', 'row')
- step_next: float32 [512], replicated
All inputs are finite; a program needn't handle non-finite values. Where the computation divides by a largest or mean magnitude, that divisor is 1e-20 or more. No bound on the sum of `creep_flag` on one device may be relied on, other than what follows from the above.
Results may differ from a plain program's by a relative error of at most 0.0035.
Values may be sent and summed in bfloat16 or wider, within the bound.
A program may use at most 64 MiB of HBM per device.

v0:
```python
import functools

import jax
import jax.numpy as jnp
from jax import lax
from jax.sharding import Mesh
from jax.sharding import PartitionSpec as P

NEWTON = 3
BLK = ("blk_0", "blk_1", "blk_2")
ROW = ("row_0", "row_1")
ROW_BLK = ("row_0", "row_1", "blk_0", "blk_1", "blk_2")


DAMPING = 0.5
PLATE_RATE = 1.0
STEP_CAP = 0.5


def in_order(parts, dim):
    dims = list(parts.shape[1:])
    dims[dim] *= parts.shape[0]
    return jnp.moveaxis(parts, 0, dim).reshape(dims)


def gather_in_order(x, axes, order):
    parts = x
    for k in order:
        parts = lax.all_gather(parts, axes[k])
    done = order[::-1]
    back = [done.index(k) for k in range(len(axes))]
    parts = parts.transpose(*back, *range(len(axes), parts.ndim))
    return parts.reshape(-1, *x.shape)


def whole_of(x, axes, order, dim):
    return in_order(gather_in_order(x, axes, order), dim)


def cut_along(x, dim, count):
    dims = x.shape
    parts = x.reshape(*dims[:dim], count, dims[dim] // count, *dims[dim + 1 :])
    return jnp.moveaxis(parts, dim, 0)


def summed_on_arrival(x, axis, dim):
    count = lax.axis_size(axis)
    parts = lax.all_to_all(cut_along(x, dim, count), axis, 0, 0, tiled=True)
    return jnp.sum(parts.astype(jnp.float32), axis=0)


def over_axes(x, axes):
    return functools.reduce(lax.pmax, axes, x)


def inverse_sinh(value):
    magnitude = jnp.abs(value)
    result = jnp.log(magnitude + jnp.sqrt(magnitude * magnitude + 1.0))
    return jnp.where(value < 0.0, -result, result)


def solve_rate(stress, pressure, rate_coef, state_coef, state, creeping):
    factor = 0.5 * jnp.exp(state_coef * jnp.log(state) / rate_coef)
    strength = pressure * rate_coef
    speed = stress / (strength * factor + DAMPING)
    for repeat in range(NEWTON):
        scaled = factor * speed
        mismatch = strength * inverse_sinh(scaled) + DAMPING * speed - stress
        gradient = strength * factor / jnp.sqrt(1.0 + scaled * scaled) + DAMPING
        speed = speed - mismatch / gradient
    return jnp.where(creeping, jnp.float32(PLATE_RATE), speed)


def advance(state, deficit, velocity, step_now):
    new_state = state * jnp.exp(step_now * (1.0 / state - jnp.abs(velocity)))
    new_deficit = deficit + step_now * (velocity - PLATE_RATE)
    return (new_state, new_deficit)


def body(
    elastic_kernel,
    slip_deficit,
    state_variable,
    step_size,
    load_stress,
    normal_stress,
    rate_table,
    evolve_table,
    patch_region,
    creep_flag,
):
    kernel_tile = elastic_kernel.reshape(elastic_kernel.shape[1], elastic_kernel.shape[3])
    elements = slip_deficit.shape[2]
    members = slip_deficit.shape[3]
    levels = jnp.arange(rate_table.shape[0], dtype=jnp.int32)
    onehot = (patch_region[..., None] == levels).astype(jnp.float32)
    rate_coef = jnp.sum(onehot * rate_table, axis=-1)[..., None]
    state_coef = jnp.sum(onehot * evolve_table, axis=-1)[..., None]
    pressure = normal_stress[..., None]
    loading = load_stress[..., None]
    creeping = (creep_flag == 1)[..., None]

    def traction_of(deficit):
        slip = deficit.astype(jnp.bfloat16)
        shards = whole_of(slip, BLK, (0, 1, 2), 0)
        breadth = shards.shape[0] * elements
        partial_sum = jnp.dot(
            kernel_tile, shards.reshape(breadth, members), preferred_element_type=jnp.float32
        )
        owned = summed_on_arrival(partial_sum.astype(jnp.bfloat16), ROW, 0)
        return owned.reshape(slip.shape)

    def velocity_of(deficit, state):
        stress = loading + traction_of(deficit)
        return solve_rate(stress, pressure, rate_coef, state_coef, state, creeping)

    deficit = slip_deficit
    state = state_variable
    step_now = step_size
    velocity = velocity_of(deficit, state)
    local_first = jnp.max(jnp.abs(velocity), axis=(0, 1, 2))
    state, deficit = advance(state, deficit, velocity, step_now)
    velocity = velocity_of(deficit, state)
    local_second = jnp.max(jnp.abs(velocity), axis=(0, 1, 2))
    maxima = over_axes(jnp.stack([local_first, local_second]), ROW_BLK)
    state, deficit = advance(state, deficit, velocity, STEP_CAP / (1.0 + maxima[0]))
    step_now = STEP_CAP / (1.0 + maxima[1])
    return (velocity, deficit, state, step_now)


def solution(mesh):
    torus = Mesh(mesh.devices.reshape(4, 2, 2, 8, 2), ("row_0", "row_1", "blk_0", "blk_1", "blk_2"))
    in_specs = (
        P(BLK, None, ROW, None),
        P(BLK, ROW, None, None),
        P(BLK, ROW, None, None),
        P(),
        P(BLK, ROW, None),
        P(BLK, ROW, None),
        P(),
        P(),
        P(BLK, ROW, None),
        P(BLK, ROW, None),
    )
    out_specs = (P(BLK, ROW, None, None), P(BLK, ROW, None, None), P(BLK, ROW, None, None), P())
    return jax.shard_map(body, mesh=torus, in_specs=in_specs, out_specs=out_specs, check_vma=False)
```

profile of v0, /device:TPU:1, one launch (start us, length us, event | category | flops | bytes accessed | tf_op | source)
XLA Modules:
  0.0 260.3 jit_solution(6911714111795193618)
XLA Ops:
  7.2 1.0 convert_element_type.22
  8.2 6.8 %all-gather = bf16[2,1,128,512]{3,2,1,0:T(8,128)(2,1)} all-gather(bf16[1,1,128,512]{3,2,1,0:T(8,128)(2,1)S(1)} %convert_element_type.22), channel_id=2, replica_groups=mesh['row_0'=4,'row_1'=2,'blk_0'=2,'blk_1'=8,'blk_2'=2] {'blk_0'}, dimensions={0}, use_global_device_ids=true | all-gather | bytes 393216 | tf_op jit(solution)/shard_map/all_gather | solution.py:29
  15.1 0.0 all-gather.13.cloned.1.call-start
  15.1 41.2 %all-gather.11.cloned.1.call-done = bf16[16,1,128,512]{3,2,1,0:T(8,128)(2,1)} async-done(((bf16[2,1,128,512]{3,2,1,0:T(8,128)(2,1)}), bf16[16,1,128,512]{3,2,1,0:T(8,128)(2,1)}) %all-gather.11.cloned.1.call-update) | async-done | bytes 2097168 | tf_op jit(solution)/shard_map/all_gather | solution.py:29
  56.4 24.3 %all-gather.13.cloned.1.call-done = bf16[16,2,1,1,128,512]{5,4,3,2,1,0:T(8,128)(2,1)} async-done(((bf16[8,2,1,1,128,512]{5,4,3,2,1,0:T(8,128)(2,1)}), bf16[16,2,1,1,128,512]{5,4,3,2,1,0:T(8,128)(2,1)}) %all-gather.13.cloned.1.call-update) | async-done | bytes 4194320 | tf_op jit(solution)/shard_map/all_gather | solution.py:29
  80.6 2.8 %copy.38 = bf16[2,8,2,1,1,128,512]{6,5,2,1,0,4,3:T(8,128)(2,1)S(1)} copy(bf16[2,8,2,1,1,128,512]{6,5,0,1,2,4,3:T(8,128)(2,1)} %bitcast.55) | data formatting | bytes 8388608 | tf_op jit(solution)/shard_map/transpose | solution.py:32
  83.4 1.8 copy-done.8
  85.3 5.5 %fusion.4 = bf16[1024,512]{1,0:T(8,128)(2,1)} fusion(bf16[4096,512]{1,0:T(8,128)(2,1)S(1)} %bitcast.57, bf16[1,1024,1,4096]{3,1,2,0:T(8,128)(2,1)S(1)} %copy-done.8), kind=kOutput, calls=%fused_computation.6 | convolution fusion | flops 4295491584 | bytes 13631488 | tf_op jit(solution)/shard_map/dot_general | solution.py:107
  90.8 4.8 %all-to-all-start = ((bf16[8,128,512]{2,1,0:T(8,128)(2,1)}), bf16[8,128,512]{2,1,0:T(8,128)(2,1)S(1)}, u32[]{:S(2)}, u32[]{:S(2)}) async-start(bf16[8,128,512]{2,1,0:T(8,128)(2,1)} %bitcast.8), calls=%async_computation | async-start | bytes 2097152 | tf_op jit(solution)/shard_map/all_to_all | solution.py:48
  95.6 0.1 select_reduce_fusion.1
  95.8 15.8 %all-to-all-done = bf16[8,128,512]{2,1,0:T(8,128)(2,1)S(1)} async-done(((bf16[8,128,512]{2,1,0:T(8,128)(2,1)}), bf16[8,128,512]{2,1,0:T(8,128)(2,1)S(1)}, u32[]{:S(2)}, u32[]{:S(2)}) %all-to-all-start) | async-done | bytes 1048608 | tf_op jit(solution)/shard_map/all_to_all | solution.py:48
  111.5 0.2 convert_reduce_fusion.1
  111.7 1.0 abs_reduce_fusion.1
  112.7 0.1 fusion.45
  112.8 6.1 %all-gather.3 = bf16[2,1,128,512]{3,2,1,0:T(8,128)(2,1)} all-gather(bf16[1,1,128,512]{3,2,1,0:T(8,128)(2,1)S(1)} %fusion.45), channel_id=5, replica_groups=mesh['row_0'=4,'row_1'=2,'blk_0'=2,'blk_1'=8,'blk_2'=2] {'blk_0'}, dimensions={0}, use_global_device_ids=true | all-gather | bytes 393216 | tf_op jit(solution)/shard_map/all_gather | solution.py:29
  118.9 0.0 all-gather.17.cloned.1.call-start
  119.0 37.6 %all-gather.15.cloned.1.call-done = bf16[16,1,128,512]{3,2,1,0:T(8,128)(2,1)} async-done(((bf16[2,1,128,512]{3,2,1,0:T(8,128)(2,1)}), bf16[16,1,128,512]{3,2,1,0:T(8,128)(2,1)}) %all-gather.15.cloned.1.call-update) | async-done | bytes 2097168 | tf_op jit(solution)/shard_map/all_gather | solution.py:29
  156.6 24.1 %all-gather.17.cloned.1.call-done = bf16[16,2,1,1,128,512]{5,4,3,2,1,0:T(8,128)(2,1)} async-done(((bf16[8,2,1,1,128,512]{5,4,3,2,1,0:T(8,128)(2,1)}), bf16[16,2,1,1,128,512]{5,4,3,2,1,0:T(8,128)(2,1)}) %all-gather.17.cloned.1.call-update) | async-done | bytes 4194320 | tf_op jit(solution)/shard_map/all_gather | solution.py:29
  180.7 2.5 copy.40
  183.2 7.1 %fusion.10 = bf16[64,8,8,128]{3,2,1,0:T(8,128)(2,1)S(1)} fusion(bf16[4096,512]{1,0:T(8,128)(2,1)S(1)} %bitcast.58, bf16[1,1024,1,4096]{3,1,2,0:T(8,128)(2,1)} %param.10), kind=kOutput, calls=%fused_computation.8 | convolution fusion | flops 4295491584 | bytes 13631488 | tf_op jit(solution)/shard_map/dot_general | solution.py:107
  190.3 0.2 copy.47
  190.5 18.8 %all_to_all.10 = bf16[8,128,512]{1,2,0:T(8,128)(2,1)S(1)} all-to-all(bf16[8,128,512]{1,2,0:T(8,128)(2,1)S(1)} %bitcast.59), channel_id=1, replica_groups=mesh['row_0'=4,'row_1'=2,'blk_0'=2,'blk_1'=8,'blk_2'=2] {'row_0','row_1'}, dimensions={0} | all-to-all | bytes 2097152 | tf_op jit(solution)/shard_map/all_to_all | solution.py:48
  209.3 0.1 convert_reduce_fusion
  209.5 0.1 copy.43
  209.6 1.0 abs_reduce_fusion
  210.7 7.0 %pmax.35 = f32[2,512]{1,0:T(2,128)S(1)} all-reduce(f32[2,512]{1,0:T(2,128)S(1)} %pad_maximum_fusion), channel_id=1, replica_groups=mesh['row_0'=4,'row_1'=2,'blk_0'=2,'blk_1'=8,'blk_2'=2] {'row_0'}, use_global_device_ids=true, to_apply=%region_6.7 | all-reduce | flops 1024 | bytes 8192 | tf_op jit(solution)/shard_map/pmax | solution.py:53
  217.7 3.8 %pmax.36 = f32[2,512]{1,0:T(2,128)S(1)} all-reduce(f32[2,512]{1,0:T(2,128)S(1)} %pmax.35), channel_id=1, replica_groups=mesh['row_0'=4,'row_1'=2,'blk_0'=2,'blk_1'=8,'blk_2'=2] {'row_1'}, use_global_device_ids=true, to_apply=%region_7.8 | all-reduce | flops 1024 | bytes 8192 | tf_op jit(solution)/shard_map/pmax | solution.py:53
  221.4 5.3 %pmax.37 = f32[2,512]{1,0:T(2,128)S(1)} all-reduce(f32[2,512]{1,0:T(2,128)S(1)} %pmax.36), channel_id=1, replica_groups=mesh['row_0'=4,'row_1'=2,'blk_0'=2,'blk_1'=8,'blk_2'=2] {'blk_0'}, use_global_device_ids=true, to_apply=%region_8.9 | all-reduce | flops 1024 | bytes 8192 | tf_op jit(solution)/shard_map/pmax | solution.py:53
  226.7 14.0 %pmax.38 = f32[2,512]{1,0:T(2,128)S(1)} all-reduce(f32[2,512]{1,0:T(2,128)S(1)} %pmax.37), channel_id=1, replica_groups=mesh['row_0'=4,'row_1'=2,'blk_0'=2,'blk_1'=8,'blk_2'=2] {'blk_1'}, use_global_device_ids=true, to_apply=%region_9.10 | all-reduce | flops 1024 | bytes 8192 | tf_op jit(solution)/shard_map/pmax | solution.py:53
  240.7 11.5 %pmax.39 = f32[2,512]{1,0:T(2,128)S(1)} all-reduce(f32[2,512]{1,0:T(2,128)S(1)} %pmax.38), channel_id=1, replica_groups=mesh['row_0'=4,'row_1'=2,'blk_0'=2,'blk_1'=8,'blk_2'=2] {'blk_2'}, use_global_device_ids=true, to_apply=%region_10.11 | all-reduce | flops 1024 | bytes 8192 | tf_op jit(solution)/shard_map/pmax | solution.py:53
  252.2 0.6 fusion.46
  252.8 1.0 exponential_multiply_fusion
  (30 shorter events, 0.2 us)
Async XLA Ops:
  7.2 49.2 %all-gather.11.cloned.1.call-start = ((), (), s32[]{:S(2)}) async-start(), calls=%async_computation.2 | async-start | bytes 2359296 | tf_op jit(solution)/shard_map/all_gather | solution.py:29
  15.1 65.6 %all-gather.13.cloned.1.call-start = ((), (), s32[]{:S(2)}) async-start(), calls=%async_computation.3 | async-start | bytes 6291456 | tf_op jit(solution)/shard_map/all_gather | solution.py:29
  80.6 4.6 %copy-start.8 = (bf16[1,1024,1,4096]{3,1,2,0:T(8,128)(2,1)S(1)}, bf16[1,1024,1,4096]{3,1,2,0:T(8,128)(2,1)}, u32[]{:S(2)}) copy-start(bf16[1,1024,1,4096]{3,1,2,0:T(8,128)(2,1)} %param.10) | copy-start | bytes 25165828
  85.3 10.3 %copy-start.4 = (f32[16]{0:T(128)S(1)}, f32[16]{0:T(128)}, u32[]{:S(2)}) copy-start(f32[16]{0:T(128)} %param.17) | copy-start | bytes 196
  85.3 10.3 %copy-start.5 = (s32[1,1,128]{2,1,0:T(1,128)S(1)}, s32[1,1,128]{2,1,0:T(1,128)}, u32[]{:S(2)}) copy-start(s32[1,1,128]{2,1,0:T(1,128)} %param.18) | copy-start | bytes 1540
  85.3 10.4 %copy-start.6 = (f32[16]{0:T(128)S(1)}, f32[16]{0:T(128)}, u32[]{:S(2)}) copy-start(f32[16]{0:T(128)} %param.16) | copy-start | bytes 196
  85.3 10.5 %copy-start.9 = (s32[1,1,128]{2,1,0:T(1,128)S(1)}, s32[1,1,128]{2,1,0:T(1,128)}, u32[]{:S(2)}) copy-start(s32[1,1,128]{2,1,0:T(1,128)} %param.19) | copy-start | bytes 1540
  85.3 10.5 %copy-start.7 = (f32[1,1,128]{2,1,0:T(1,128)S(1)}, f32[1,1,128]{2,1,0:T(1,128)}, u32[]{:S(2)}) copy-start(f32[1,1,128]{2,1,0:T(1,128)} %param.15) | copy-start | bytes 1540
  85.3 26.4 %copy-start.1 = (f32[1,1,128,512]{3,2,1,0:T(8,128)S(1)}, f32[1,1,128,512]{3,2,1,0:T(8,128)}, u32[]{:S(2)}) copy-start(f32[1,1,128,512]{3,2,1,0:T(8,128)} %param.12) | copy-start | bytes 786436
  85.3 26.4 %copy-start.10 = (f32[1,1,128]{2,1,0:T(1,128)S(1)}, f32[1,1,128]{2,1,0:T(1,128)}, u32[]{:S(2)}) copy-start(f32[1,1,128]{2,1,0:T(1,128)} %param.14) | copy-start | bytes 1540
  90.8 21.9 %copy-start = (f32[1,1,128,512]{3,2,1,0:T(8,128)S(1)}, f32[1,1,128,512]{3,2,1,0:T(8,128)}, u32[]{:S(2)}) copy-start(f32[1,1,128,512]{3,2,1,0:T(8,128)} %param.11) | copy-start | bytes 786436
  90.8 21.9 %copy-start.3 = (f32[512]{0:T(512)S(1)}, f32[512]{0:T(512)}, u32[]{:S(2)}) copy-start(f32[512]{0:T(512)} %param.13) | copy-start | bytes 6148
  90.8 20.7 %all-to-all-start = ((bf16[8,128,512]{2,1,0:T(8,128)(2,1)}), bf16[8,128,512]{2,1,0:T(8,128)(2,1)S(1)}, u32[]{:S(2)}, u32[]{:S(2)}) async-start(bf16[8,128,512]{2,1,0:T(8,128)(2,1)} %bitcast.8), calls=%async_computation | async-start | bytes 2097152 | tf_op jit(solution)/shard_map/all_to_all | solution.py:48
  95.6 61.0 %all-gather.15.cloned.1.call-start = ((), (), s32[]{:S(2)}) async-start(), calls=%async_computation.4 | async-start | bytes 2359296 | tf_op jit(solution)/shard_map/all_gather | solution.py:29
  118.9 61.8 %all-gather.17.cloned.1.call-start = ((), (), s32[]{:S(2)}) async-start(), calls=%async_computation.5 | async-start | bytes 6291456 | tf_op jit(solution)/shard_map/all_gather | solution.py:29
  210.7 43.1 %copy-start.2 = (f32[1,1,128,512]{3,2,1,0:T(8,128)}, f32[1,1,128,512]{3,2,1,0:T(8,128)S(1)}, u32[]{:S(2)}) copy-start(f32[1,1,128,512]{3,2,1,0:T(8,128)S(1)} %get-tuple-element.13) | copy-start | bytes 786436
Sparse Core Ops, SparseCore 0:
  15.2 41.1 all-gather.10
  58.1 22.4 all-gather.12
  119.0 37.4 all-gather.14
  158.2 22.4 all-gather.16
where the time goes:
time: 261 us; the launch traced here: 260 us
  waiting for transfers between devices  143 us (55%)
  blocking collectives  73.2 us (28%)
  between operations  13.9 us (5%)
  matrix products  12.6 us (5%)
  local copies, waits for them, and re-layouts  7.45 us (3%)
  other arithmetic  5.04 us (2%)
  starting transfers between devices  4.93 us (2%)
    all_gather x4, waiting for transfers between devices, gather_in_order(): parts = lax.all_gather(parts, axes[k])  127 us
    pmax x5, blocking collectives, over_axes(): return functools.reduce(lax.pmax, axes, x)  41.5 us
    all_to_all x1, blocking collectives, summed_on_arrival(): parts = lax.all_to_all(cut_along(x, dim, count), axis, 0, 0, tiled=True)  18.8 us
    all_to_all x1, waiting for transfers between devices, summed_on_arrival(): parts = lax.all_to_all(cut_along(x, dim, count), axis, 0, 0, tiled=True)  15.8 us
    all_gather x2, blocking collectives, gather_in_order(): parts = lax.all_gather(parts, axes[k])  12.9 us
    dot_general x2, matrix products, traction_of(): jnp.dot(kernel_tile, shards.reshape(breadth, members), preferred_element_...  12.6 us
    transpose x2, local copies, waits for them, and re-layouts, gather_in_order(): parts = parts.transpose(*back, *range(len(axes), parts.ndim))  5.24 us
  transfers between devices with their start and end apart: 5, of which 5 were waited for; matrix products, arithmetic and copies ran while one was open for 0% of the time, Pallas kernels for 0%

commit v1 on v0

v1 whole, which is shorter than its diff:
```python
import functools

import jax
import jax.numpy as jnp
from jax import lax
from jax.experimental import pallas as pl
from jax.experimental.pallas import tpu as pltpu
from jax.sharding import Mesh
from jax.sharding import PartitionSpec as P

NEWTON = 3
DAMPING = 0.5
PLATE_RATE = 1.0
STEP_CAP = 0.5

AXES = ("row_0", "row_1", "blk_0", "blk_1", "blk_2")
BLK = ("blk_0", "blk_1", "blk_2")
ROW = ("row_0", "row_1")
MESH = pl.DeviceIdType.MESH

CHUNKS = 2
E = 128
ORDER = (0, 7, 1, 6, 2, 5, 3, 4)
GROUPS = ((0, 4), (4, 12), (12, 20), (20, 32))


def slot(plane, offset, core):
    return ORDER.index(offset) * 4 + plane * 2 + core


def kernel_body(
    k_hbm,
    deficit_hbm,
    state_hbm,
    step_hbm,
    load_hbm,
    normal_hbm,
    rate_hbm,
    evolve_hbm,
    region_hbm,
    creep_hbm,
    v_out,
    d_out,
    s_out,
    step_out,
    kv,
    gathered,
    acc,
    own_sum,
    xsend,
    xrecv,
    ysend,
    yrecv,
    deficit,
    state,
    factor,
    vel,
    step_in,
    load_in,
    normal_in,
    rate_in,
    evolve_in,
    region_in,
    creep_in,
    cols,
    top,
    mid,
    top_recv,
    mid_recv,
    step_fin,
    k_sem,
    in_sem,
    out_sem,
    send_sem,
    recv_sem,
    max_send,
    max_recv,
):
    members = deficit.shape[1]
    width = members // CHUNKS
    x = lax.axis_index("row_0")
    yl = lax.axis_index("row_1")
    yh = lax.axis_index("blk_0")
    z = lax.axis_index("blk_1")
    core = lax.axis_index("blk_2")

    z_up = {"blk_1": lax.rem(z + 1, 8)}
    z_down = {"blk_1": lax.rem(z + 7, 8)}
    y_far = {"blk_0": 1 - yh}
    sibling = {"blk_2": 1 - core}
    y_near = {"row_1": 1 - yl}
    x_peer = {k: {"row_0": lax.rem(x + k, 4)} for k in (1, 2, 3)}
    plane_peers = [
        {"row_0": lax.rem(x + dx, 4), "row_1": (yl + dl) % 2, "blk_0": (yh + dh) % 2}
        for dx in range(4)
        for dl in range(2)
        for dh in range(2)
        if dx or dl or dh
    ]
    line_peers = [
        {"blk_1": lax.rem(z + dz, 8), "blk_2": (core + dc) % 2}
        for dz in range(8)
        for dc in range(2)
        if dz or dc
    ]

    loads = []
    for i, (src, dst) in enumerate(
        (
            (deficit_hbm, deficit),
            (step_hbm, step_in),
            (load_hbm, load_in),
            (normal_hbm, normal_in),
            (rate_hbm, rate_in),
            (evolve_hbm, evolve_in),
            (region_hbm, region_in),
            (creep_hbm, creep_in),
            (state_hbm, state),
        )
    ):
        copy = pltpu.make_async_copy(src, dst, in_sem.at[i])
        copy.start()
        loads.append(copy)

    barrier = pltpu.get_barrier_semaphore()
    for peer in plane_peers + line_peers:
        pl.semaphore_signal(barrier, inc=1, device_id=peer, device_id_type=MESH)

    for group, (low, high) in enumerate(GROUPS):
        for at in range(low, high):
            offset, plane, cr = ORDER[at // 4], (at // 2) % 2, at % 2
            block = (((yh + plane) % 2) * 8 + lax.rem(z + offset, 8)) * 2 + (core + cr) % 2
            pltpu.make_async_copy(
                k_hbm.at[:, pl.ds(pl.multiple_of(block * E, E), E)],
                kv.at[:, pl.ds(at * E, E)],
                k_sem.at[group],
            ).start()

    sent = []
    flight = {}

    def send(phase, key, src, dst, number, device):
        copy = pltpu.make_async_remote_copy(
            src_ref=src,
            dst_ref=dst,
            send_sem=send_sem.at[phase, number],
            recv_sem=recv_sem.at[phase, number],
            device_id=device,
            device_id_type=MESH,
        )
        copy.start()
        sent.append(copy)
        flight[(phase, key)] = copy

    def arrived(phase, *keys):
        for key in keys:
            flight[(phase, key)].wait_recv()

    def rows_of(phase, at, half=None):
        if half is None:
            return gathered.at[phase, pl.ds(at * E, E)]
        return gathered.at[phase, pl.ds(at * E + half * (E // 2), E // 2)]

    numbers = {}

    def number_of(key):
        return numbers.setdefault(key, len(numbers))

    def move(phase, plane, offset, to_plane, to_offset, device, half=None):
        key = (to_plane, to_offset, half)
        send(
            phase,
            key,
            rows_of(phase, slot(plane, offset, 0), half),
            rows_of(phase, slot(to_plane, to_offset, 0), half),
            number_of(key),
            device,
        )

    def share(phase, plane, offset):
        key = ("core", plane, offset)
        send(
            phase,
            key,
            rows_of(phase, slot(plane, offset, 0)),
            rows_of(phase, slot(plane, offset, 1)),
            number_of(key),
            sibling,
        )

    def shared(phase, *blocks):
        arrived(phase, *(("core", plane, offset) for plane, offset in blocks))

    def round_0(phase):
        move(phase, 0, 0, 0, 7, z_up)
        move(phase, 0, 0, 0, 1, z_down)
        move(phase, 0, 0, 1, 0, y_far)
        share(phase, 0, 0)

    def round_1(phase):
        arrived(phase, (0, 7, None))
        move(phase, 0, 7, 0, 6, z_up)
        arrived(phase, (0, 1, None))
        move(phase, 0, 1, 0, 2, z_down)
        arrived(phase, (1, 0, None))
        move(phase, 1, 0, 1, 7, z_up)
        move(phase, 1, 0, 1, 1, z_down)
        share(phase, 1, 0)
        share(phase, 0, 7)
        share(phase, 0, 1)

    def round_2(phase):
        arrived(phase, (0, 6, None))
        move(phase, 0, 6, 0, 5, z_up)
        move(phase, 0, 6, 1, 6, y_far, 1)
        arrived(phase, (0, 2, None))
        move(phase, 0, 2, 0, 3, z_down)
        move(phase, 0, 2, 1, 2, y_far, 1)
        arrived(phase, (1, 7, None))
        move(phase, 1, 7, 1, 6, z_up, 0)
        arrived(phase, (1, 1, None))
        move(phase, 1, 1, 1, 2, z_down, 0)
        share(phase, 0, 6)
        share(phase, 0, 2)
        share(phase, 1, 7)
        share(phase, 1, 1)

    def round_3(phase):
        arrived(phase, (0, 5, None))
        move(phase, 0, 5, 0, 4, z_up, 0)
        move(phase, 0, 5, 1, 5, y_far)
        arrived(phase, (0, 3, None))
        move(phase, 0, 3, 0, 4, z_down, 1)
        move(phase, 0, 3, 1, 3, y_far)
        share(phase, 0, 5)
        share(phase, 0, 3)
        arrived(phase, (1, 6, 0), (1, 6, 1))
        share(phase, 1, 6)
        arrived(phase, (1, 2, 0), (1, 2, 1))
        share(phase, 1, 2)

    def round_4(phase):
        arrived(phase, (0, 4, 0), (0, 4, 1))
        move(phase, 0, 4, 1, 4, y_far)
        share(phase, 0, 4)
        arrived(phase, (1, 5, None))
        share(phase, 1, 5)
        arrived(phase, (1, 3, None))
        share(phase, 1, 3)
        arrived(phase, (1, 4, None))
        share(phase, 1, 4)

    def product(phase, group, rows):
        low, high = GROUPS[group]
        return jnp.dot(
            kv[rows, low * E : high * E],
            gathered[phase, low * E : high * E, :],
            preferred_element_type=jnp.float32,
        )

    def multiply(phase, chunk, group):
        if phase == 0:
            low, high = GROUPS[group]
            part = kv.at[:, pl.ds(low * E, (high - low) * E)]
            pltpu.make_async_copy(part, part, k_sem.at[group]).wait()

        def tile(i, carry):
            rows = pl.ds(pl.multiple_of(i * 256, 256), 256)
            value = product(phase, group, rows)
            if group == 0:
                acc[chunk, rows] = value
            else:
                acc[chunk, rows] += value
            return carry

        lax.fori_loop(0, 4, tile, 0)

    def multiply_last(phase, chunk):
        group = len(GROUPS) - 1
        if phase == 0:
            low, high = GROUPS[group]
            part = kv.at[:, pl.ds(low * E, (high - low) * E)]
            pltpu.make_async_copy(part, part, k_sem.at[group]).wait()
        for dx in (2, 1, 3, 0):
            rows = pl.ds(pl.multiple_of(lax.rem(x + dx, 4) * 256, 256), 256)
            value = acc[chunk, rows] + product(phase, group, rows)
            if dx:
                xsend[phase, dx - 1] = value.astype(jnp.bfloat16)
                send(
                    phase,
                    ("x", dx),
                    xsend.at[phase, dx - 1],
                    xrecv.at[phase, dx - 1],
                    number_of(("x", dx)),
                    x_peer[dx],
                )
            else:
                own_sum[chunk] = value

    def reduce_x(phase, chunk):
        arrived(phase, ("x", 1), ("x", 2), ("x", 3))
        other = pl.multiple_of((1 - yl) * E, E)
        mine = pl.multiple_of(yl * E, E)

        def tile(i, carry):
            for base, target in ((other, 0), (mine, 1)):
                rows = pl.ds(pl.multiple_of(base + i * 32, 32), 32)
                total = own_sum[chunk, rows]
                for k in range(3):
                    total = total + xrecv[phase, k, rows].astype(jnp.float32)
                if target == 0:
                    ysend[phase, pl.ds(pl.multiple_of(i * 32, 32), 32)] = total.astype(jnp.bfloat16)
                else:
                    own_sum[chunk, rows] = total
            return carry

        lax.fori_loop(0, 4, tile, 0)
        send(phase, "y", ysend.at[phase], yrecv.at[phase], number_of("y"), y_near)

    def set_factor(chunk):
        lanes = slice(chunk * width, (chunk + 1) * width)

        def tile(i, carry):
            rows = pl.ds(pl.multiple_of(i * 32, 32), 32)
            rate = cols[rows, 2:3]
            evolve = cols[rows, 3:4]
            factor[chunk, rows] = 0.5 * jnp.exp(evolve * jnp.log(state[rows, lanes]) / rate)
            return carry

        lax.fori_loop(0, 4, tile, 0)

    def solve(phase, chunk, step):
        lanes = slice(chunk * width, (chunk + 1) * width)
        mine = pl.multiple_of(yl * E, E)
        arrived(phase, "y")
        step_now = step_in[:, lanes]

        def tile(i, carry):
            rows = pl.ds(pl.multiple_of(i * 32, 32), 32)
            from_rows = pl.ds(pl.multiple_of(mine + i * 32, 32), 32)
            loading = cols[rows, 0:1]
            strength = cols[rows, 1:2] * cols[rows, 2:3]
            creeping = cols[rows, 4:5]
            stress = loading + (own_sum[chunk, from_rows] + yrecv[phase, rows].astype(jnp.float32))
            scale = factor[chunk, rows]
            slope = strength * scale
            speed = stress / (slope + DAMPING)
            for _ in range(NEWTON):
                scaled = scale * speed
                magnitude = jnp.abs(scaled)
                root = jnp.sqrt(magnitude * magnitude + 1.0)
                arc = jnp.log(magnitude + root)
                arc = jnp.where(scaled < 0.0, -arc, arc)
                mismatch = strength * arc + DAMPING * speed - stress
                gradient = slope / root + DAMPING
                speed = speed - mismatch / gradient
            speed = jnp.where(creeping > 0.5, jnp.float32(PLATE_RATE), speed)
            size = jnp.abs(speed)
            if step == 0:
                old = state[rows, lanes]
                state[rows, lanes] = old * jnp.exp(step_now * (1.0 / old - size))
                moved = deficit[rows, lanes] + step_now * (speed - PLATE_RATE)
                deficit[rows, lanes] = moved
                gathered[phase + CHUNKS, pl.ds(pl.multiple_of(i * 32, 32), 32)] = moved.astype(jnp.bfloat16)
            else:
                vel[rows, lanes] = speed
            return jnp.maximum(carry, jnp.max(size.reshape(4, 8, width), axis=0))

        largest = lax.fori_loop(0, 4, tile, jnp.zeros((8, width), jnp.float32))
        top[step, :, lanes] = jnp.max(largest, axis=0, keepdims=True)

    max_copies = {}

    def max_send_all(step, stage):
        peers = plane_peers if stage == 0 else line_peers
        source = top if stage == 0 else mid
        target = top_recv if stage == 0 else mid_recv
        copies = []
        for k, peer in enumerate(peers):
            copy = pltpu.make_async_remote_copy(
                src_ref=source.at[step],
                dst_ref=target.at[step, k],
                send_sem=max_send.at[step, stage, k],
                recv_sem=max_recv.at[step, stage, k],
                device_id=peer,
                device_id_type=MESH,
            )
            copy.start()
            copies.append(copy)
            sent.append(copy)
        max_copies[(step, stage)] = copies

    def max_take(step, stage):
        for copy in max_copies[(step, stage)]:
            copy.wait_recv()
        source = top if stage == 0 else mid
        target = top_recv if stage == 0 else mid_recv
        return jnp.maximum(source[step], jnp.max(target[step], axis=0))

    loads[0].wait()
    for chunk in range(CHUNKS):
        gathered[chunk, 0:E] = deficit[:, chunk * width : (chunk + 1) * width].astype(jnp.bfloat16)
    for copy in loads[1:]:
        copy.wait()
    region = region_in[...]
    rate_row = jnp.zeros((1, E), jnp.float32)
    evolve_row = jnp.zeros((1, E), jnp.float32)
    for level in range(rate_in.shape[1]):
        chosen = region == level
        rate_row = jnp.where(chosen, rate_in[:, level : level + 1], rate_row)
        evolve_row = jnp.where(chosen, evolve_in[:, level : level + 1], evolve_row)
    creep_row = jnp.where(creep_in[...] == 1, 1.0, 0.0).astype(jnp.float32)
    picked = lax.broadcasted_iota(jnp.int32, (E, E), 0)
    stacked = jnp.zeros((E, E), jnp.float32)
    for k, row in enumerate((load_in[...], normal_in[...], rate_row, evolve_row, creep_row)):
        stacked = jnp.where(picked == k, jnp.broadcast_to(row, (E, E)), stacked)
    cols[...] = stacked.T

    pl.semaphore_wait(barrier, len(plane_peers) + len(line_peers))

    first = list(range(CHUNKS))
    for chunk in first:
        round_0(chunk)
    for chunk in first:
        set_factor(chunk)

    for step in range(2):
        phases = [step * CHUNKS + chunk for chunk in range(CHUNKS)]
        for chunk, phase in enumerate(phases):
            round_1(phase)
        for chunk, phase in enumerate(phases):
            round_2(phase)
            shared(phase, (0, 0), (1, 0))
            multiply(phase, chunk, 0)
        for chunk, phase in enumerate(phases):
            round_3(phase)
            shared(phase, (0, 7), (0, 1), (1, 7), (1, 1))
            multiply(phase, chunk, 1)
            if step == 1 and chunk == 0:
                mid[0] = max_take(0, 0)
                max_send_all(0, 1)
        for chunk, phase in enumerate(phases):
            round_4(phase)
            shared(phase, (0, 6), (0, 2), (1, 6), (1, 2))
            multiply(phase, chunk, 2)
            shared(phase, (0, 5), (0, 3), (0, 4), (1, 5), (1, 3), (1, 4))
            multiply_last(phase, chunk)
        for chunk, phase in enumerate(phases):
            reduce_x(phase, chunk)
        for chunk, phase in enumerate(phases):
            solve(phase, chunk, step)
            if step == 0:
                round_0(phase + CHUNKS)
        max_send_all(step, 0)
        if step == 0:
            for chunk in range(CHUNKS):
                set_factor(chunk)

    outs = []

    def put(src, dst, i):
        copy = pltpu.make_async_copy(src, dst, out_sem.at[i])
        copy.start()
        outs.append(copy)

    put(vel, v_out, 0)
    step_last = STEP_CAP / (1.0 + max_take(0, 1))

    def finish(i, carry):
        rows = pl.ds(pl.multiple_of(i * 16, 16), 16)
        speed = vel[rows]
        old = state[rows]
        state[rows] = old * jnp.exp(step_last * (1.0 / old - jnp.abs(speed)))
        deficit[rows] = deficit[rows] + step_last * (speed - PLATE_RATE)
        return carry

    lax.fori_loop(0, 8, finish, 0)
    put(deficit, d_out, 1)
    put(state, s_out, 2)
    mid[1] = max_take(1, 0)
    max_send_all(1, 1)
    step_fin[...] = STEP_CAP / (1.0 + max_take(1, 1))
    put(step_fin, step_out, 3)
    for copy in outs:
        copy.wait()
    for copy in sent:
        copy.wait_send()


def body(
    elastic_kernel,
    slip_deficit,
    state_variable,
    step_size,
    load_stress,
    normal_stress,
    rate_table,
    evolve_table,
    patch_region,
    creep_flag,
):
    members = slip_deficit.shape[3]
    width = members // CHUNKS
    phases = 2 * CHUNKS
    regions = rate_table.shape[0]
    f32, bf16, i32 = jnp.float32, jnp.bfloat16, jnp.int32
    anywhere = pl.BlockSpec(memory_space=pl.ANY)
    whole = jax.ShapeDtypeStruct((E, members), f32)
    scratch = [
        pltpu.VMEM((1024, 4096), bf16),
        pltpu.VMEM((phases, 4096, width), bf16),
        pltpu.VMEM((CHUNKS, 1024, width), f32),
        pltpu.VMEM((CHUNKS, 256, width), f32),
        pltpu.VMEM((phases, 3, 256, width), bf16),
        pltpu.VMEM((phases, 3, 256, width), bf16),
        pltpu.VMEM((phases, E, width), bf16),
        pltpu.VMEM((phases, E, width), bf16),
        pltpu.VMEM((E, members), f32),
        pltpu.VMEM((E, members), f32),
        pltpu.VMEM((CHUNKS, E, width), f32),
        pltpu.VMEM((E, members), f32),
        pltpu.VMEM((1, members), f32),
        pltpu.VMEM((1, E), f32),
        pltpu.VMEM((1, E), f32),
        pltpu.VMEM((1, regions), f32),
        pltpu.VMEM((1, regions), f32),
        pltpu.VMEM((1, E), i32),
        pltpu.VMEM((1, E), i32),
        pltpu.VMEM((E, E), f32),
        pltpu.VMEM((2, 1, members), f32),
        pltpu.VMEM((2, 1, members), f32),
        pltpu.VMEM((2, 15, 1, members), f32),
        pltpu.VMEM((2, 15, 1, members), f32),
        pltpu.VMEM((1, members), f32),
        pltpu.SemaphoreType.DMA((len(GROUPS),)),
        pltpu.SemaphoreType.DMA((9,)),
        pltpu.SemaphoreType.DMA((4,)),
        pltpu.SemaphoreType.DMA((phases, 40)),
        pltpu.SemaphoreType.DMA((phases, 40)),
        pltpu.SemaphoreType.DMA((2, 2, 15)),
        pltpu.SemaphoreType.DMA((2, 2, 15)),
    ]
    velocity, deficit, state, step_next = pl.pallas_call(
        kernel_body,
        out_shape=(whole, whole, whole, jax.ShapeDtypeStruct((1, members), f32)),
        in_specs=[anywhere] * 10,
        out_specs=(anywhere,) * 4,
        scratch_shapes=scratch,
        compiler_params=pltpu.CompilerParams(
            collective_id=0, has_side_effects=True, vmem_limit_bytes=60 * 1024 * 1024
        ),
        name="fault_steps",
    )(
        elastic_kernel.reshape(1024, 4096),
        slip_deficit.reshape(E, members),
        state_variable.reshape(E, members),
        step_size.reshape(1, members),
        load_stress.reshape(1, E),
        normal_stress.reshape(1, E),
        rate_table.reshape(1, regions),
        evolve_table.reshape(1, regions),
        patch_region.reshape(1, E),
        creep_flag.reshape(1, E),
    )
    shape = slip_deficit.shape
    return velocity.reshape(shape), deficit.reshape(shape), state.reshape(shape), step_next.reshape(members)


def solution(mesh):
    torus = Mesh(mesh.devices.reshape(4, 2, 2, 8, 2), AXES)
    in_specs = (
        P(BLK, None, ROW, None),
        P(BLK, ROW, None, None),
        P(BLK, ROW, None, None),
        P(),
        P(BLK, ROW, None),
        P(BLK, ROW, None),
        P(),
        P(),
        P(BLK, ROW, None),
        P(BLK, ROW, None),
    )
    out_specs = (P(BLK, ROW, None, None), P(BLK, ROW, None, None), P(BLK, ROW, None, None), P())
    return jax.shard_map(body, mesh=torus, in_specs=in_specs, out_specs=out_specs, check_vma=False)
```

time: 261 us -> 118 us (0.45)
  waiting for transfers between devices: 143 us -> 0 us
  Pallas kernels: 0 us -> 111 us
  blocking collectives: 73.2 us -> 0 us
  between operations: 13.9 us -> 0.64 us
  matrix products: 12.6 us -> 0 us
  other arithmetic: 5.04 us -> 0 us
  starting transfers between devices: 4.93 us -> 0 us
    all_gather x4 -> x0, waiting for transfers between devices: 127 us -> none  [gather_in_order(): parts = lax.all_gather(parts, axes[k])]
    pallas_call x0 -> x1, Pallas kernels: none -> 111 us  [body(): pl.pallas_call(kernel_body, out_shape=(whole, whole, whole, jax.ShapeDtyp...]
    pmax x5 -> x0, blocking collectives: 41.5 us -> none  [over_axes(): return functools.reduce(lax.pmax, axes, x)]
    all_to_all x1 -> x0, blocking collectives: 18.8 us -> none  [summed_on_arrival(): parts = lax.all_to_all(cut_along(x, dim, count), axis, 0, 0, tiled=True)]
    all_to_all x1 -> x0, waiting for transfers between devices: 15.8 us -> none  [summed_on_arrival(): parts = lax.all_to_all(cut_along(x, dim, count), axis, 0, 0, tiled=True)]
    all_gather x2 -> x0, blocking collectives: 12.9 us -> none  [gather_in_order(): parts = lax.all_gather(parts, axes[k])]
    dot_general x2 -> x0, matrix products: 12.6 us -> none  [traction_of(): jnp.dot(kernel_tile, shards.reshape(breadth, members), preferred_element_...]
    transpose x2 -> x0, local copies, waits for them, and re-layouts: 5.24 us -> none  [gather_in_order(): parts = parts.transpose(*back, *range(len(axes), parts.ndim))]
  transfers between devices with their start and end apart: 5 -> 0, of which waited for: 5 -> 0; matrix products, arithmetic and copies ran while one was open for 0% -> 0% of each run, Pallas kernels for 0% -> 0%
where the time goes in v1:
time: 118 us
  Pallas kernels  111 us (94%)
  local copies, waits for them, and re-layouts  6.26 us (5%)
    pallas_call x1, Pallas kernels, body(): pl.pallas_call(kernel_body, out_shape=(whole, whole, whole, jax.ShapeDtyp...  111 us
    unnamed x4, local copies, waits for them, and re-layouts  6.26 us

profile of v1, /device:TPU:1, one launch (start us, length us, event | category | flops | bytes accessed | tf_op | source)
XLA Modules:
  0.0 117.8 jit_solution(7586223907786762050)
XLA Ops:
  0.6 110.9 %fault_steps.1 = (f32[128,512]{1,0:T(8,128)}, f32[128,512]{1,0:T(8,128)}, f32[128,512]{1,0:T(8,128)}, f32[1,512]{1,0:T(1,128)}) custom-call(bf16[1024,4096]{1,0:T(8,128)(2,1)} %bitcast.14, f32[128,512]{1,0:T(8,128)} %bitcast.15, f32[128,512]{1,0:T(8,128)} %bitcast.16, f32[1,512]{1,0:T(1,128)} %bitcast.20, f32[1,128]{1,0:T(1,128)} %bitcast.22, ...), custom_call_target="tpu_custom_call" | custom-call | tf_op jit(solution)/shard_map/fault_steps/pallas_call | solution.py:543
  111.5 1.7 %copy.18 = f32[1,1,128,512]{3,2,1,0:T(8,128)} copy(f32[1,1,128,512]{3,2,1,0:T(8,128)} %bitcast.19) | data formatting | bytes 524288
  113.2 1.7 %copy.19 = f32[1,1,128,512]{3,2,1,0:T(8,128)} copy(f32[1,1,128,512]{3,2,1,0:T(8,128)} %bitcast.18) | data formatting | bytes 524288
  114.9 1.7 %copy.20 = f32[1,1,128,512]{3,2,1,0:T(8,128)} copy(f32[1,1,128,512]{3,2,1,0:T(8,128)} %bitcast.17) | data formatting | bytes 524288
  116.5 1.3 %copy.21 = f32[512]{0:T(512)} copy(f32[512]{0:T(512)} %bitcast.21) | data formatting | bytes 4096

commit v2 on v1

v2 whole, which is shorter than its diff:
```python
import functools
import itertools

import jax
import jax.numpy as jnp
from jax import lax
from jax.experimental import pallas as pl
from jax.experimental.pallas import tpu as pltpu
from jax.sharding import Mesh
from jax.sharding import PartitionSpec as P

NEWTON = 3
DAMPING = 0.5
PLATE_RATE = 1.0
STEP_CAP = 0.5

AXES = ("row_0", "row_1", "blk_0", "blk_1", "blk_2")
BLK = ("blk_0", "blk_1", "blk_2")
ROW = ("row_0", "row_1")
MESH = pl.DeviceIdType.MESH

CHUNKS = 2
E = 128
TILE = 64
ROW_OFFSETS = ((2, 1), (2, 0), (1, 1), (3, 1), (1, 0), (3, 0), (0, 1))
OFFSETS = ((0,), (7, 1), (6, 2), (5, 3, 4))
GROUPS = ((0, 4), (4, 12), (12, 20), (20, 32))


LIMIT = 62


def slot(plane, offset, core):
    group = next(g for g, offsets in enumerate(OFFSETS) if offset in offsets)
    offsets = OFFSETS[group]
    return GROUPS[group][0] + (core * 2 + plane) * len(offsets) + offsets.index(offset)


def kernel_body(
    k_hbm,
    deficit_hbm,
    state_hbm,
    step_hbm,
    load_hbm,
    normal_hbm,
    rate_hbm,
    evolve_hbm,
    region_hbm,
    creep_hbm,
    v_out,
    d_out,
    s_out,
    step_out,
    kv,
    gathered,
    acc,
    xsend,
    xrecv,
    deficit,
    state,
    factor,
    step_in,
    load_in,
    normal_in,
    rate_in,
    evolve_in,
    region_in,
    creep_in,
    cols,
    top,
    mid,
    top_recv,
    mid_recv,
    k_sem,
    in_sem,
    send_sem,
    recv_sem,
    max_send,
    max_recv,
):
    members = deficit.shape[1]
    width = members // CHUNKS
    x = lax.axis_index("row_0")
    yl = lax.axis_index("row_1")
    yh = lax.axis_index("blk_0")
    z = lax.axis_index("blk_1")
    core = lax.axis_index("blk_2")

    z_up = {"blk_1": lax.rem(z + 1, 8)}
    z_down = {"blk_1": lax.rem(z + 7, 8)}
    y_far = {"blk_0": 1 - yh}
    sibling = {"blk_2": 1 - core}
    plane_peers = [
        {"row_0": lax.rem(x + dx, 4), "row_1": (yl + dl) % 2, "blk_0": (yh + dh) % 2}
        for dx in range(4)
        for dl in range(2)
        for dh in range(2)
        if dx or dl or dh
    ]
    line_peers = [
        {"blk_1": lax.rem(z + dz, 8), "blk_2": (core + dc) % 2}
        for dz in range(8)
        for dc in range(2)
        if dz or dc
    ]

    loads = []
    for i, (src, dst) in enumerate(
        (
            (deficit_hbm, deficit),
            (step_hbm, step_in),
            (load_hbm, load_in),
            (normal_hbm, normal_in),
            (rate_hbm, rate_in),
            (evolve_hbm, evolve_in),
            (region_hbm, region_in),
            (creep_hbm, creep_in),
            (state_hbm, state),
        )
    ):
        copy = pltpu.make_async_copy(src, dst, in_sem.at[i])
        copy.start()
        loads.append(copy)

    barrier = pltpu.get_barrier_semaphore()
    first_peers = [z_up, z_down, y_far, sibling] + [
        {"row_0": lax.rem(x + dx, 4), "row_1": (yl + dl) % 2} for dx, dl in ROW_OFFSETS
    ]
    for peer in first_peers:
        pl.semaphore_signal(barrier, inc=1, device_id=peer, device_id_type=MESH)

    for group, (low, high) in enumerate(GROUPS):
        for offset, plane, cr in itertools.product(OFFSETS[group], range(2), range(2)):
            at = slot(plane, offset, cr)
            block = (((yh + plane) % 2) * 8 + lax.rem(z + offset, 8)) * 2 + (core + cr) % 2
            pltpu.make_async_copy(
                k_hbm.at[:, pl.ds(pl.multiple_of(block * E, E), E)],
                kv.at[:, pl.ds(at * E, E)],
                k_sem.at[group],
            ).start()

    sent = []
    flight = {}

    def send(phase, key, src, dst, number, device):
        copy = pltpu.make_async_remote_copy(
            src_ref=src,
            dst_ref=dst,
            send_sem=send_sem.at[phase, number],
            recv_sem=recv_sem.at[phase, number],
            device_id=device,
            device_id_type=MESH,
        )
        copy.start()
        sent.append(copy)
        flight[(phase, key)] = copy

    def arrived(phase, *keys):
        for key in keys:
            flight[(phase, key)].wait_recv()

    def rows_of(phase, at, half=None):
        if half is None:
            return gathered.at[phase, pl.ds(at * E, E)]
        return gathered.at[phase, pl.ds(at * E + half * (E // 2), E // 2)]

    numbers = {}

    def number_of(key):
        return numbers.setdefault(key, len(numbers))

    def move(phase, plane, offset, to_plane, to_offset, device, half=None):
        key = (to_plane, to_offset, half)
        send(
            phase,
            key,
            rows_of(phase, slot(plane, offset, 0), half),
            rows_of(phase, slot(to_plane, to_offset, 0), half),
            number_of(key),
            device,
        )

    def share(phase, plane, *offsets):
        key = ("core", plane, offsets)
        at, to, count = slot(plane, offsets[0], 0), slot(plane, offsets[0], 1), len(offsets) * E
        send(
            phase,
            key,
            gathered.at[phase, pl.ds(at * E, count)],
            gathered.at[phase, pl.ds(to * E, count)],
            number_of(key),
            sibling,
        )

    def shared(phase, *parts):
        for offsets in parts:
            arrived(phase, ("core", 0, offsets), ("core", 1, offsets))

    def round_0(phase):
        move(phase, 0, 0, 0, 7, z_up)
        move(phase, 0, 0, 0, 1, z_down)
        move(phase, 0, 0, 1, 0, y_far)
        share(phase, 0, 0)

    def round_1(phase):
        arrived(phase, (0, 7, None))
        move(phase, 0, 7, 0, 6, z_up)
        move(phase, 0, 7, 1, 7, y_far, 1)
        arrived(phase, (0, 1, None))
        move(phase, 0, 1, 0, 2, z_down)
        move(phase, 0, 1, 1, 1, y_far, 1)
        arrived(phase, (1, 0, None))
        move(phase, 1, 0, 1, 7, z_up, 0)
        move(phase, 1, 0, 1, 1, z_down, 0)
        share(phase, 0, 7, 1)
        share(phase, 1, 0)

    def round_2(phase):
        arrived(phase, (0, 6, None))
        move(phase, 0, 6, 0, 5, z_up)
        move(phase, 0, 6, 1, 6, y_far, 1)
        arrived(phase, (0, 2, None))
        move(phase, 0, 2, 0, 3, z_down)
        move(phase, 0, 2, 1, 2, y_far, 1)
        arrived(phase, (1, 7, 0))
        move(phase, 1, 7, 1, 6, z_up, 0)
        arrived(phase, (1, 1, 0))
        move(phase, 1, 1, 1, 2, z_down, 0)
        share(phase, 0, 6, 2)
        arrived(phase, (1, 7, 1), (1, 1, 1))
        share(phase, 1, 7, 1)

    def round_3(phase):
        arrived(phase, (0, 5, None))
        move(phase, 0, 5, 0, 4, z_up, 0)
        move(phase, 0, 5, 1, 5, y_far, 1)
        arrived(phase, (0, 3, None))
        move(phase, 0, 3, 0, 4, z_down, 1)
        move(phase, 0, 3, 1, 3, y_far, 1)
        arrived(phase, (1, 6, 0))
        move(phase, 1, 6, 1, 5, z_up, 0)
        arrived(phase, (1, 2, 0))
        move(phase, 1, 2, 1, 3, z_down, 0)
        share(phase, 0, 5, 3)
        arrived(phase, (1, 6, 1), (1, 2, 1))
        share(phase, 1, 6, 2)

    def round_4(phase):
        arrived(phase, (0, 4, 1))
        move(phase, 0, 4, 1, 4, y_far, 1)
        arrived(phase, (1, 5, 0))
        move(phase, 1, 5, 1, 4, z_up, 0)
        arrived(phase, (0, 4, 0))
        share(phase, 0, 4)
        arrived(phase, (1, 3, 0), (1, 3, 1), (1, 5, 1))
        share(phase, 1, 5, 3)

    def round_5(phase):
        arrived(phase, (1, 4, 0), (1, 4, 1))
        share(phase, 1, 4)

    def product(phase, group):
        low, high = GROUPS[group]
        return jnp.dot(
            kv[:, low * E : high * E],
            gathered[phase, low * E : high * E, :],
            preferred_element_type=jnp.float32,
        )

    def multiply(phase, chunk, group):
        if phase == 0:
            low, high = GROUPS[group]
            part = kv.at[:, pl.ds(low * E, (high - low) * E)]
            pltpu.make_async_copy(part, part, k_sem.at[group]).wait()

        value = product(phase, group)
        if group == 0:
            acc[chunk] = value
        else:
            acc[chunk] += value

    def multiply_last(phase, chunk):
        multiply(phase, chunk, len(GROUPS) - 1)
        for k, (dx, dl) in enumerate(ROW_OFFSETS):
            base = (lax.rem(x + dx, 4) * 2 + (yl + dl) % 2) * E

            def tile(i, carry):
                rows = pl.ds(pl.multiple_of(base + i * 64, 64), 64)
                xsend[phase, k, pl.ds(pl.multiple_of(i * 64, 64), 64)] = acc[chunk, rows].astype(jnp.bfloat16)
                return carry

            lax.fori_loop(0, 2, tile, 0)
            send(
                phase,
                ("row", k),
                xsend.at[phase, k],
                xrecv.at[phase, k],
                number_of(("row", k)),
                {"row_0": lax.rem(x + dx, 4), "row_1": (yl + dl) % 2},
            )

    def set_factor(chunk):
        lanes = slice(chunk * width, (chunk + 1) * width)

        def tile(i, carry):
            rows = pl.ds(pl.multiple_of(i * 32, 32), 32)
            rate = cols[rows, 2:3]
            evolve = cols[rows, 3:4]
            factor[chunk, rows] = 0.5 * jnp.exp(evolve * jnp.log(state[rows, lanes]) / rate)
            return carry

        lax.fori_loop(0, 4, tile, 0)

    def solve(phase, chunk, step):
        lanes = slice(chunk * width, (chunk + 1) * width)
        arrived(phase, *(("row", k) for k in range(7)))
        own = (x * 2 + yl) * E
        step_now = step_in[:, lanes]

        def tile(i, carry):
            rows = pl.ds(pl.multiple_of(i * TILE, TILE), TILE)
            loading = cols[rows, 0:1]
            strength = cols[rows, 1:2] * cols[rows, 2:3]
            creeping = cols[rows, 4:5]
            total = acc[chunk, pl.ds(pl.multiple_of(own + i * TILE, TILE), TILE)]
            for k in range(7):
                total = total + xrecv[phase, k, rows].astype(jnp.float32)
            stress = loading + total
            scale = factor[chunk, rows]
            slope = strength * scale
            speed = stress / (slope + DAMPING)
            for _ in range(NEWTON):
                scaled = scale * speed
                magnitude = jnp.abs(scaled)
                root = jnp.sqrt(magnitude * magnitude + 1.0)
                arc = jnp.log(magnitude + root)
                arc = jnp.where(scaled < 0.0, -arc, arc)
                mismatch = strength * arc + DAMPING * speed - stress
                gradient = slope / root + DAMPING
                speed = speed - mismatch / gradient
            speed = jnp.where(creeping > 0.5, jnp.float32(PLATE_RATE), speed)
            size = jnp.abs(speed)
            if step == 0:
                old = state[rows, lanes]
                state[rows, lanes] = old * jnp.exp(step_now * (1.0 / old - size))
                moved = deficit[rows, lanes] + step_now * (speed - PLATE_RATE)
                deficit[rows, lanes] = moved
                gathered[phase + CHUNKS, pl.ds(pl.multiple_of(i * TILE, TILE), TILE)] = moved.astype(jnp.bfloat16)
            else:
                v_out[rows, lanes] = speed
            return jnp.maximum(carry, jnp.max(size.reshape(TILE // 8, 8, width), axis=0))

        largest = lax.fori_loop(0, E // TILE, tile, jnp.zeros((8, width), jnp.float32))
        top[step, :, lanes] = jnp.max(largest, axis=0, keepdims=True)

    max_copies = {}

    def max_send_all(step, stage):
        peers = plane_peers if stage == 0 else line_peers
        source = top if stage == 0 else mid
        target = top_recv if stage == 0 else mid_recv
        copies = []
        for k, peer in enumerate(peers):
            copy = pltpu.make_async_remote_copy(
                src_ref=source.at[step],
                dst_ref=target.at[step, k],
                send_sem=max_send.at[step, stage, k],
                recv_sem=max_recv.at[step, stage, k],
                device_id=peer,
                device_id_type=MESH,
            )
            copy.start()
            copies.append(copy)
            sent.append(copy)
        max_copies[(step, stage)] = copies

    def max_take(step, stage):
        for copy in max_copies[(step, stage)]:
            copy.wait_recv()
        source = top if stage == 0 else mid
        target = top_recv if stage == 0 else mid_recv
        return jnp.maximum(source[step], jnp.max(target[step], axis=0))

    outs = []
    loads[0].wait()
    for chunk in range(CHUNKS):
        gathered[chunk, 0:E] = deficit[:, chunk * width : (chunk + 1) * width].astype(jnp.bfloat16)
    for copy in loads[1:]:
        copy.wait()
    region = region_in[...]
    rate_row = jnp.zeros((1, E), jnp.float32)
    evolve_row = jnp.zeros((1, E), jnp.float32)
    for level in range(rate_in.shape[1]):
        chosen = region == level
        rate_row = jnp.where(chosen, rate_in[:, level : level + 1], rate_row)
        evolve_row = jnp.where(chosen, evolve_in[:, level : level + 1], evolve_row)
    creep_row = jnp.where(creep_in[...] == 1, 1.0, 0.0).astype(jnp.float32)
    picked = lax.broadcasted_iota(jnp.int32, (E, E), 0)
    stacked = jnp.zeros((E, E), jnp.float32)
    for k, row in enumerate((load_in[...], normal_in[...], rate_row, evolve_row, creep_row)):
        stacked = jnp.where(picked == k, jnp.broadcast_to(row, (E, E)), stacked)
    cols[...] = stacked.T

    pl.semaphore_wait(barrier, len(first_peers))

    first = list(range(CHUNKS))
    for chunk in first:
        round_0(chunk)
    for chunk in first:
        set_factor(chunk)

    for step in range(2):
        phases = [step * CHUNKS + chunk for chunk in range(CHUNKS)]
        def stage(k, chunk):
            phase = phases[chunk]
            if k == 1:
                round_1(phase)
            elif k == 2:
                round_2(phase)
                shared(phase, (0,))
                multiply(phase, chunk, 0)
            elif k == 3:
                round_3(phase)
                shared(phase, (7, 1))
                multiply(phase, chunk, 1)
                if step == 1 and chunk == 0:
                    mid[0] = max_take(0, 0)
                    max_send_all(0, 1)
            elif k == 4:
                round_4(phase)
                shared(phase, (6, 2))
                multiply(phase, chunk, 2)
            elif k == 5:
                round_5(phase)
                shared(phase, (5, 3), (4,))
                multiply_last(phase, chunk)
            elif k == 6:
                solve(phase, chunk, step)
                if step == 0:
                    round_0(phase + CHUNKS)

        plan = sorted((k, chunk, k) for k in range(1, 7) for chunk in range(CHUNKS))
        for _, chunk, k in plan:
            stage(k, chunk)
        max_send_all(step, 0)
        if step == 0:
            for chunk in range(CHUNKS):
                set_factor(chunk)


    step_last = STEP_CAP / (1.0 + max_take(0, 1))

    def finish(i, carry):
        rows = pl.ds(pl.multiple_of(i * 16, 16), 16)
        speed = v_out[rows]
        old = state[rows]
        s_out[rows] = old * jnp.exp(step_last * (1.0 / old - jnp.abs(speed)))
        d_out[rows] = deficit[rows] + step_last * (speed - PLATE_RATE)
        return carry

    lax.fori_loop(0, 8, finish, 0)
    mid[1] = max_take(1, 0)
    max_send_all(1, 1)
    step_out[...] = STEP_CAP / (1.0 + max_take(1, 1))
    for copy in sent:
        copy.wait_send()


def body(
    elastic_kernel,
    slip_deficit,
    state_variable,
    step_size,
    load_stress,
    normal_stress,
    rate_table,
    evolve_table,
    patch_region,
    creep_flag,
):
    members = slip_deficit.shape[3]
    width = members // CHUNKS
    phases = 2 * CHUNKS
    regions = rate_table.shape[0]
    f32, bf16, i32 = jnp.float32, jnp.bfloat16, jnp.int32
    anywhere = pl.BlockSpec(memory_space=pl.ANY)
    whole = pltpu.VMEM((E, members), f32)
    scratch = [
        pltpu.VMEM((1024, 4096), bf16),
        pltpu.VMEM((phases, 4096, width), bf16),
        pltpu.VMEM((CHUNKS, 1024, width), f32),
        pltpu.VMEM((phases, 7, E, width), bf16),
        pltpu.VMEM((phases, 7, E, width), bf16),
        pltpu.VMEM((E, members), f32),
        pltpu.VMEM((E, members), f32),
        pltpu.VMEM((CHUNKS, E, width), f32),
        pltpu.VMEM((1, members), f32),
        pltpu.VMEM((1, E), f32),
        pltpu.VMEM((1, E), f32),
        pltpu.VMEM((1, regions), f32),
        pltpu.VMEM((1, regions), f32),
        pltpu.VMEM((1, E), i32),
        pltpu.VMEM((1, E), i32),
        pltpu.VMEM((E, E), f32),
        pltpu.VMEM((2, 1, members), f32),
        pltpu.VMEM((2, 1, members), f32),
        pltpu.VMEM((2, 15, 1, members), f32),
        pltpu.VMEM((2, 15, 1, members), f32),
        pltpu.SemaphoreType.DMA((len(GROUPS),)),
        pltpu.SemaphoreType.DMA((9,)),
        pltpu.SemaphoreType.DMA((phases, 48)),
        pltpu.SemaphoreType.DMA((phases, 48)),
        pltpu.SemaphoreType.DMA((2, 2, 15)),
        pltpu.SemaphoreType.DMA((2, 2, 15)),
    ]
    velocity, deficit, state, step_next = pl.pallas_call(
        kernel_body,
        out_shape=(whole, whole, whole, pltpu.VMEM((1, members), f32)),
        in_specs=[anywhere] * 10,
        out_specs=(pl.BlockSpec(memory_space=pltpu.VMEM),) * 4,
        scratch_shapes=scratch,
        compiler_params=pltpu.CompilerParams(
            collective_id=0, has_side_effects=True, vmem_limit_bytes=LIMIT * 1024 * 1024
        ),
        name="fault_steps",
    )(
        elastic_kernel.reshape(1024, 4096),
        slip_deficit.reshape(E, members),
        state_variable.reshape(E, members),
        step_size.reshape(1, members),
        load_stress.reshape(1, E),
        normal_stress.reshape(1, E),
        rate_table.reshape(1, regions),
        evolve_table.reshape(1, regions),
        patch_region.reshape(1, E),
        creep_flag.reshape(1, E),
    )
    shape = slip_deficit.shape
    return velocity.reshape(shape), deficit.reshape(shape), state.reshape(shape), step_next.reshape(members)


def solution(mesh):
    torus = Mesh(mesh.devices.reshape(4, 2, 2, 8, 2), AXES)
    in_specs = (
        P(BLK, None, ROW, None),
        P(BLK, ROW, None, None),
        P(BLK, ROW, None, None),
        P(),
        P(BLK, ROW, None),
        P(BLK, ROW, None),
        P(),
        P(),
        P(BLK, ROW, None),
        P(BLK, ROW, None),
    )
    out_specs = (P(BLK, ROW, None, None), P(BLK, ROW, None, None), P(BLK, ROW, None, None), P())
    return jax.shard_map(body, mesh=torus, in_specs=in_specs, out_specs=out_specs, check_vma=False)
```

time: 118 us -> 99.4 us (0.84)
  Pallas kernels: 111 us -> 96 us
  local copies, waits for them, and re-layouts: 6.26 us -> 2.69 us
    pallas_call x1, Pallas kernels: 111 us -> 96 us  [body(): pl.pallas_call(kernel_body, out_shape=(whole, whole, whole, pltpu.VMEM((1...]
    unnamed x4, local copies, waits for them, and re-layouts: 6.26 us -> 2.69 us
where the time goes in v2:
time: 99.4 us; the launch traced here: 99.3 us
  Pallas kernels  96 us (97%)
  local copies, waits for them, and re-layouts  2.69 us (3%)
    pallas_call x1, Pallas kernels, body(): pl.pallas_call(kernel_body, out_shape=(whole, whole, whole, pltpu.VMEM((1...  96 us
    unnamed x4, local copies, waits for them, and re-layouts  2.69 us

profile of v2, /device:TPU:1, one launch (start us, length us, event | category | flops | bytes accessed | tf_op | source)
XLA Modules:
  0.0 99.3 jit_solution(11843815446063777922)
XLA Ops:
  0.6 96.0 %fault_steps.1 = (f32[128,512]{1,0:T(8,128)S(1)}, f32[128,512]{1,0:T(8,128)S(1)}, f32[128,512]{1,0:T(8,128)S(1)}, f32[1,512]{1,0:T(1,128)S(1)}) custom-call(bf16[1024,4096]{1,0:T(8,128)(2,1)} %bitcast.18, f32[128,512]{1,0:T(8,128)} %bitcast.19, f32[128,512]{1,0:T(8,128)} %bitcast.20, f32[1,512]{1,0:T(1,128)} %bitcast.21, f32[1,128]{1,0:T(1,128)} %bitcast.22, ...), custom_call_target="tpu_custom_call" | custom-call | tf_op jit(solution)/shard_map/fault_steps/pallas_call | solution.py:516
  96.6 0.7 copy.18
  97.3 0.7 copy.19
  98.0 0.6 copy.21
  98.6 0.7 copy.20

commit v3 on v2

--- a/solution.py
+++ b/solution.py
@@ -336,8 +336,7 @@
                 arc = jnp.log(magnitude + root)
                 arc = jnp.where(scaled < 0.0, -arc, arc)
                 mismatch = strength * arc + DAMPING * speed - stress
-                gradient = slope / root + DAMPING
-                speed = speed - mismatch / gradient
+                speed = speed - mismatch * root / (slope + DAMPING * root)
             speed = jnp.where(creeping > 0.5, jnp.float32(PLATE_RATE), speed)
             size = jnp.abs(speed)
             if step == 0:

time: 99.4 us -> 99.4 us (level)
  no operation moved by 1% of the time
where the time goes in v3:
time: 99.4 us; the launch traced here: 99.3 us
  Pallas kernels  96 us (97%)
  local copies, waits for them, and re-layouts  2.69 us (3%)
    pallas_call x1, Pallas kernels, body(): pl.pallas_call(kernel_body, out_shape=(whole, whole, whole, pltpu.VMEM((1...  96 us
    unnamed x4, local copies, waits for them, and re-layouts  2.69 us

profile of v3, /device:TPU:1, one launch (start us, length us, event | category | flops | bytes accessed | tf_op | source)
XLA Modules:
  0.0 99.3 jit_solution(14449614527384683353)
XLA Ops:
  0.6 96.0 %fault_steps.1 = (f32[128,512]{1,0:T(8,128)S(1)}, f32[128,512]{1,0:T(8,128)S(1)}, f32[128,512]{1,0:T(8,128)S(1)}, f32[1,512]{1,0:T(1,128)S(1)}) custom-call(bf16[1024,4096]{1,0:T(8,128)(2,1)} %bitcast.18, f32[128,512]{1,0:T(8,128)} %bitcast.19, f32[128,512]{1,0:T(8,128)} %bitcast.20, f32[1,512]{1,0:T(1,128)} %bitcast.21, f32[1,128]{1,0:T(1,128)} %bitcast.22, ...), custom_call_target="tpu_custom_call" | custom-call | tf_op jit(solution)/shard_map/fault_steps/pallas_call | solution.py:515
  96.6 0.7 copy.18
  97.3 0.7 copy.19
  98.1 0.6 copy.21
  98.6 0.7 copy.20
